TPU v7x, 32 devices: a whole 2x2x4 slice. The times are simulated.
32 devices in a mesh: dev: 32 (over z, y, x, core).
Axes of the slice: x: 2, y: 2, z: 4, core: 2. Of those that a mesh axis runs over, the one named last changes fastest.
Arguments:
- state: float32 [128, 512, 128], P('dev'), may hold values from -6 to 6
- background: float32 [128, 512, 128], P('dev'), may hold values from -6 to 6
- back_precision: float32 [128], replicated, may hold values from 0.2 to 2
- conv_first: bfloat16 [3, 3, 128, 128], replicated, may hold values from -0.1875 to 0.1875
- bias_first: float32 [128], replicated, may hold values from -3 to 3
- conv_second: bfloat16 [3, 3, 128, 128], replicated, may hold values from -0.1875 to 0.1875
- sounding_tile: int32 [16384, 1], P('dev'), may hold values from 0 to 31; in each aligned block of 512 rows (0 to 511, 512 to 1023, ...) at most 32 rows name the same one
- sounding_cells: int32 [16384, 4], P('dev'), may hold values from 0 to 2047
- cell_weights: float32 [16384, 4], P('dev'), may hold values from 0.1 to 1
- observations: float32 [16384, 616], P('dev'), may hold values from -6 to 6
- live_counts: int32 [32], P('dev'), may hold values from 1 to 511, as said below
- layer_in: bfloat16 [128, 1024], replicated, may hold values from -0.5 to 0.5
- bias_in: float32 [1024], replicated, may hold values from -3 to 3
- layer_out: bfloat16 [1024, 616], replicated, may hold values from -0.1875 to 0.1875
- bias_out: float32 [616], replicated, may hold values from -3 to 3
- error_precision: float32 [616, 616], replicated, as said below
Outputs:
- gradient: float32 [128, 512, 128], P('dev')
Inputs may be any that keep to these rules, and one draw needn't show every extreme that they name: `sounding_tile`: among the 512 soundings of one list, at most 32 lie in the same strip, and in some lists some strip holds exactly 32 of them. The live soundings of a list are its first live_counts; the counts of lists l and l + 16 sum to 512. `error_precision`: Symmetric.
All inputs are finite; a program needn't handle non-finite values.
Results may differ from a plain program's by a relative error of at most 0.008.
Values may be sent and summed in bfloat16 or wider, within the bound.
A program may use at most 64 MiB of HBM per device.

v0:
```python
import jax
import jax.numpy as jnp
from jax import lax
from jax.sharding import PartitionSpec as P


def padded_2(block, sides, width):
    for axis, dim in sides:
        count = lax.axis_size(axis)
        forward = [(i, i + 1) for i in range(count - 1)]
        backward = [(target, source) for source, target in forward]
        low = lax.ppermute(
            lax.slice_in_dim(block, block.shape[dim] - width, None, axis=dim), axis, forward
        )
        high = lax.ppermute(lax.slice_in_dim(block, 0, width, axis=dim), axis, backward)
        block = jnp.concatenate([low, block, high], axis=dim)
    return block


def conv_rows(padded, kernel):
    tile_rows = padded.shape[0] - 2
    channels = padded.shape[2]
    total = jnp.zeros((tile_rows * padded.shape[1], kernel.shape[3]), jnp.float32)
    for row_off in range(3):
        row_band = padded[row_off : row_off + tile_rows]
        for col_off in range(3):
            shifted = jnp.roll(row_band, 1 - col_off, axis=1)
            total = total + jnp.dot(
                shifted.reshape(-1, channels),
                kernel[row_off, col_off],
                preferred_element_type=jnp.float32,
            )
    return total.reshape(tile_rows, padded.shape[1], kernel.shape[3])


def rim_conv(field_in, kernel):
    padded = padded_2(field_in, (("dev", 0),), 1)
    return conv_rows(padded, kernel)


def flipped(kernel):
    return kernel[::-1, ::-1].transpose(0, 1, 3, 2)


def network_adjoint(
    interpolated, measured, live_mask, layer_in, bias_in, layer_out, bias_out, error_precision
):
    pre_act = jnp.dot(interpolated, layer_in, preferred_element_type=jnp.float32) + bias_in
    activated = jnp.tanh(pre_act).astype(jnp.bfloat16)
    radiance = jnp.dot(activated, layer_out, preferred_element_type=jnp.float32) + bias_out
    innovation = (radiance - measured) * live_mask[:, None]
    weighted = jnp.dot(innovation, error_precision, precision=lax.Precision.HIGHEST)
    back_act = jnp.dot(
        weighted.astype(jnp.bfloat16), layer_out.T, preferred_element_type=jnp.float32
    )
    act_wide = activated.astype(jnp.float32)
    pre_grad = (back_act * (1.0 - act_wide * act_wide)).astype(jnp.bfloat16)
    return jnp.dot(pre_grad, layer_in.T, preferred_element_type=jnp.float32)


def per_device(
    state,
    background,
    back_precision,
    conv_first,
    bias_first,
    conv_second,
    sounding_tile,
    sounding_cells,
    cell_weights,
    observations,
    live_counts,
    layer_in,
    bias_in,
    layer_out,
    bias_out,
    error_precision,
):
    tile_rows, tile_cols, channels = state.shape
    devices = lax.axis_size("dev")
    listed = sounding_tile.shape[0]
    capacity = 2 * listed // devices
    margin = sounding_cells.shape[1]
    state_bf = state.astype(jnp.bfloat16)
    hidden = jnp.tanh(rim_conv(state_bf, conv_first) + bias_first).astype(jnp.bfloat16)
    observed = (state + rim_conv(hidden, conv_second)).astype(jnp.bfloat16)
    observed_flat = observed.reshape(-1, channels)
    owners = sounding_tile[:, 0]
    one_hot = (owners[:, None] == jnp.arange(devices, dtype=jnp.int32)[None, :]).astype(jnp.int32)
    ranking = jnp.sum((jnp.cumsum(one_hot, axis=0) - one_hot) * one_hot, axis=1)
    slot_of = owners * capacity + ranking
    requests = jnp.zeros((devices * capacity, margin), jnp.int32).at[slot_of].set(sounding_cells)
    requested = lax.all_to_all(
        requests.reshape(devices, capacity, margin), "dev", split_axis=0, concat_axis=0, tiled=True
    )
    picked = observed_flat[requested.reshape(-1)].reshape(devices, capacity, margin, channels)
    wanted = jnp.zeros((devices * capacity, margin), jnp.float32).at[slot_of].set(cell_weights)
    shares = lax.all_to_all(
        wanted.reshape(devices, capacity, margin), "dev", split_axis=0, concat_axis=0, tiled=True
    )
    blended = jnp.sum(picked.astype(jnp.float32) * shares[..., None], axis=2).astype(jnp.bfloat16)
    returned = lax.all_to_all(blended, "dev", split_axis=0, concat_axis=0, tiled=True)
    interpolated = returned.reshape(devices * capacity, channels)[slot_of]
    live_here = live_counts[0]
    live_mask = (jnp.arange(listed, dtype=jnp.int32) < live_here).astype(jnp.float32)
    sounding_grad = network_adjoint(
        interpolated,
        observations,
        live_mask,
        layer_in,
        bias_in,
        layer_out,
        bias_out,
        error_precision,
    )
    outgoing = jnp.zeros((devices * capacity, channels), jnp.float32).at[slot_of].set(sounding_grad)
    arrived = lax.all_to_all(
        outgoing.reshape(devices, capacity, channels).astype(jnp.bfloat16),
        "dev",
        split_axis=0,
        concat_axis=0,
        tiled=True,
    ).astype(jnp.float32)
    flat_terms = (arrived[:, :, None, :] * shares[..., None]).reshape(-1, channels)
    obs_grad = (
        jnp.zeros((tile_rows * tile_cols, channels), jnp.float32)
        .at[requested.reshape(-1)]
        .add(flat_terms)
    )
    obs_grad = obs_grad.reshape(tile_rows, tile_cols, channels)
    hid_grad = rim_conv(obs_grad.astype(jnp.bfloat16), flipped(conv_second))
    hidden_wide = hidden.astype(jnp.float32)
    act_grad = (hid_grad * (1.0 - hidden_wide * hidden_wide)).astype(jnp.bfloat16)
    model_grad = rim_conv(act_grad, flipped(conv_first))
    return obs_grad + model_grad + back_precision * (state - background)


def solution(mesh):
    return jax.shard_map(
        per_device,
        mesh=mesh,
        in_specs=(
            P("dev", None, None),
            P("dev", None, None),
            P(),
            P(),
            P(),
            P(),
            P("dev", None),
            P("dev", None),
            P("dev", None),
            P("dev", None),
            P("dev"),
            P(),
            P(),
            P(),
            P(),
            P(),
        ),
        out_specs=P("dev", None, None),
        check_vma=False,
    )
```

profile of v0, /device:TPU:15, one launch (start us, length us, event | category | flops | bytes accessed | tf_op | source)
XLA Modules:
  0.0 180.3 jit_solution(6512066576312565851)
XLA Ops:
  0.0 1.4 convert_element_type.78
  1.5 3.7 %collective-permute-start = (bf16[1,512,128]{2,1,0:T(8,128)(2,1)S(1)}, bf16[1,512,128]{2,1,0:T(8,128)(2,1)S(1)}, u32[]{:S(2)}, u32[]{:S(2)}) collective-permute-start(bf16[1,512,128]{2,1,0:T(8,128)(2,1)S(1)} %get-tuple-element.86), channel_id=1, source_target_pairs={{0,1},{1,2},{2,3},{3,4},{4,5},{5,6},{6,7},{7,8},{8,9},{9,10},{10,1... | collective-permute-start | bytes 393224 | tf_op jit(solution)/shard_map/ppermute | solution.py:12
  5.2 1.9 %collective-permute-start.1 = (bf16[1,512,128]{2,1,0:T(8,128)(2,1)S(1)}, bf16[1,512,128]{2,1,0:T(8,128)(2,1)S(1)}, u32[]{:S(2)}, u32[]{:S(2)}) collective-permute-start(bf16[1,512,128]{2,1,0:T(8,128)(2,1)S(1)} %get-tuple-element.85), channel_id=1, source_target_pairs={{1,0},{2,1},{3,2},{4,3},{5,4},{6,5},{7,6},{8,7},{9,8},{10,9},{11,1... | collective-permute-start | bytes 393224 | tf_op jit(solution)/shard_map/ppermute | solution.py:15
  7.1 1.2 reduce-window.6
  8.8 1.8 %scatter_custom_fusion = s32[1024,4]{1,0:T(8,128)S(1)} fusion(s32[512]{0:T(512)S(1)} %bitcast.290, s32[512,4]{1,0:T(8,128)S(1)} %copy.21, s32[]{:T(128)} %constant.7.clone.1), kind=kCustom, calls=%fused_computation.178 | custom fusion | bytes 16388 | tf_op jit(solution)/shard_map/scatter | solution.py:92
  10.9 0.7 reshape.297
  11.7 6.2 %all-to-all-start = ((s32[32,1,128]{2,1,0:T(1,128)}), s32[32,1,128]{2,1,0:T(1,128)S(1)}, u32[]{:S(2)}, u32[]{:S(2)}) async-start(s32[32,1,128]{2,1,0:T(1,128)} %reshape.297), calls=%async_computation | async-start | bytes 32768 | tf_op jit(solution)/shard_map/all_to_all | solution.py:93
  18.1 1.8 %scatter_custom_fusion.1 = f32[1024,4]{1,0:T(8,128)S(1)} fusion(s32[512]{0:T(512)S(1)} %bitcast.291, f32[512,4]{1,0:T(8,128)S(1)} %copy.24, f32[]{:T(128)} %constant.6.clone.1), kind=kCustom, calls=%fused_computation.174 | custom fusion | bytes 16388 | tf_op jit(solution)/shard_map/scatter | solution.py:97
  20.2 0.7 reshape.299
  20.9 0.8 all-to-all-done
  21.7 5.8 %all-to-all-start.1 = ((f32[32,1,128]{2,1,0:T(1,128)}), f32[32,1,128]{2,1,0:T(1,128)S(1)}, u32[]{:S(2)}, u32[]{:S(2)}) async-start(f32[32,1,128]{2,1,0:T(1,128)} %reshape.299), calls=%async_computation.1 | async-start | bytes 32768 | tf_op jit(solution)/shard_map/all_to_all | solution.py:98
  27.5 0.5 broadcast.80
  28.0 0.7 reduce.2
  29.4 1.9 %all-to-all-done.1 = f32[32,1,128]{2,1,0:T(1,128)S(1)} async-done(((f32[32,1,128]{2,1,0:T(1,128)}), f32[32,1,128]{2,1,0:T(1,128)S(1)}, u32[]{:S(2)}, u32[]{:S(2)}) %all-to-all-start.1) | async-done | bytes 16416 | tf_op jit(solution)/shard_map/all_to_all | solution.py:98
  31.9 0.7 reduce.3
  32.7 1.1 copy.26
  34.3 1.6 fusion.45
  39.0 4.6 %collective-permute-start.2 = (bf16[1,512,128]{2,1,0:T(8,128)(2,1)S(1)}, bf16[1,512,128]{2,1,0:T(8,128)(2,1)S(1)}, u32[]{:S(2)}, u32[]{:S(2)}) collective-permute-start(bf16[1,512,128]{2,1,0:T(8,128)(2,1)S(1)} %get-tuple-element.75), channel_id=1, source_target_pairs={{0,1},{1,2},{2,3},{3,4},{4,5},{5,6},{6,7},{7,8},{8,9},{9,10},{10,1... | collective-permute-start | bytes 393224 | tf_op jit(solution)/shard_map/ppermute | solution.py:12
  43.6 2.1 %collective-permute-start.3 = (bf16[1,512,128]{2,1,0:T(8,128)(2,1)S(1)}, bf16[1,512,128]{2,1,0:T(8,128)(2,1)S(1)}, u32[]{:S(2)}, u32[]{:S(2)}) collective-permute-start(bf16[1,512,128]{2,1,0:T(8,128)(2,1)S(1)} %get-tuple-element.74), channel_id=1, source_target_pairs={{1,0},{2,1},{3,2},{4,3},{5,4},{6,5},{7,6},{8,7},{9,8},{10,9},{11,1... | collective-permute-start | bytes 393224 | tf_op jit(solution)/shard_map/ppermute | solution.py:15
  45.8 5.9 %collective-permute-done.3 = bf16[1,512,128]{2,1,0:T(8,128)(2,1)S(1)} collective-permute-done((bf16[1,512,128]{2,1,0:T(8,128)(2,1)S(1)}, bf16[1,512,128]{2,1,0:T(8,128)(2,1)S(1)}, u32[]{:S(2)}, u32[]{:S(2)}) %collective-permute-start.3) | collective-permute-done | bytes 131104 | tf_op jit(solution)/shard_map/ppermute | solution.py:15
  55.9 0.9 copy-done.2
  57.0 15.0 %gather_fusion = bf16[4096,128]{1,0:T(8,128)(2,1)} fusion(bf16[2048,128]{1,0:T(8,128)(2,1)S(1)} %bitcast.235, s32[4096]{0:T(1024)S(1)} %broadcast_clamp_fusion), kind=kCustom, calls=%fused_computation | custom fusion | bytes 2113536 | tf_op jit(solution)/shard_map/gather | solution.py:96
  72.0 4.0 %fusion.1 = bf16[32,32,128]{2,1,0:T(8,128)(2,1)} fusion(bf16[32,32,4,128]{3,2,1,0:T(4,128)(2,1)} %bitcast.246, f32[32,32,4]{2,1,0:T(8,128)} %copy.26), kind=kLoop, calls=%fused_computation.40 | loop fusion | flops 1441792 | bytes 1327104 | tf_op jit(solution)/shard_map/reduce_sum | solution.py:101
  76.1 3.7 %all-to-all-start.2 = ((bf16[32,32,128]{2,1,0:T(8,128)(2,1)}), bf16[32,32,128]{2,1,0:T(8,128)(2,1)S(1)}, u32[]{:S(2)}, u32[]{:S(2)}) async-start(bf16[32,32,128]{2,1,0:T(8,128)(2,1)} %fusion.1), calls=%async_computation.2 | async-start | bytes 524288 | tf_op jit(solution)/shard_map/all_to_all | solution.py:102
  80.4 6.9 %all-to-all-done.2 = bf16[32,32,128]{2,1,0:T(8,128)(2,1)S(1)} async-done(((bf16[32,32,128]{2,1,0:T(8,128)(2,1)}), bf16[32,32,128]{2,1,0:T(8,128)(2,1)S(1)}, u32[]{:S(2)}, u32[]{:S(2)}) %all-to-all-start.2) | async-done | bytes 262176 | tf_op jit(solution)/shard_map/all_to_all | solution.py:102
  87.3 1.3 gather_fusion.1
  88.7 1.4 tanh_convert_fusion
  90.1 1.0 copy-done.19
  91.0 2.6 %fusion.5 = f32[512,616]{0,1:T(8,128)S(1)} fusion(f32[512,616]{0,1:T(8,128)} %param.25, bf16[512,1024]{1,0:T(8,128)(2,1)S(1)} %tanh_convert_fusion, bf16[1024,616]{0,1:T(8,128)(2,1)} %param.29, f32[512]{0:T(512)S(1)} %fusion.101, f32[616]{0:T(1024)S(1)} %copy-done.18), kind=kOutput, calls=%fused_computation.47 | convolution fusion | flops 646868992 | bytes 4837792 | tf_op jit(solution)/shard_map/dot_general | solution.py:50
  93.6 3.2 %convolution_convert_fusion = bf16[512,616]{0,1:T(8,128)(2,1)S(1)} fusion(f32[512,616]{0,1:T(8,128)S(1)} %fusion.5, f32[616,616]{1,0:T(8,128)S(1)} %copy-done), kind=kOutput, calls=%fused_computation.48 | convolution fusion | flops 2331693056 | bytes 3410176 | tf_op jit(solution)/shard_map/dot_general | solution.py:52
  96.8 3.2 %fusion.6 = f32[512,128]{1,0:T(8,128)S(1)} fusion(bf16[128,1024]{1,0:T(8,128)(2,1)} %param.27, bf16[512,1024]{1,0:T(8,128)(2,1)} %copy-done.19, bf16[512,616]{0,1:T(8,128)(2,1)S(1)} %convolution_convert_fusion, bf16[1024,616]{0,1:T(8,128)(2,1)} %param.29), kind=kOutput, calls=%fused_computation.49 | convolution fusion | flops 782761984 | bytes 3465216 | tf_op jit(solution)/shard_map/dot_general | solution.py:58
  100.0 1.8 %scatter_custom_fusion.2 = f32[1024,128]{1,0:T(8,128)S(1)} fusion(s32[512]{0:T(512)S(1)} %bitcast.293, f32[512,128]{1,0:T(8,128)S(1)} %fusion.6, f32[]{:T(128)} %constant.6.clone.1), kind=kCustom, calls=%fused_computation.176 | custom fusion | bytes 524292 | tf_op jit(solution)/shard_map/scatter | solution.py:116
  101.9 0.7 convert_element_type.90
  102.6 5.6 %all-to-all-start.3 = ((bf16[32,32,128]{2,1,0:T(8,128)(2,1)}), bf16[32,32,128]{2,1,0:T(8,128)(2,1)S(1)}, u32[]{:S(2)}, u32[]{:S(2)}) async-start(bf16[32,32,128]{2,1,0:T(8,128)(2,1)} %bitcast.49), calls=%async_computation.3 | async-start | bytes 524288 | tf_op jit(solution)/shard_map/all_to_all | solution.py:117
  108.2 0.7 reverse_bitcast_fusion.1
  109.2 6.5 %all-to-all-done.3 = bf16[32,32,128]{2,1,0:T(8,128)(2,1)S(1)} async-done(((bf16[32,32,128]{2,1,0:T(8,128)(2,1)}), bf16[32,32,128]{2,1,0:T(8,128)(2,1)S(1)}, u32[]{:S(2)}, u32[]{:S(2)}) %all-to-all-start.3) | async-done | bytes 262176 | tf_op jit(solution)/shard_map/all_to_all | solution.py:117
  115.8 1.8 %mul.79 = f32[32,32,4,128]{3,2,1,0:T(4,128)} broadcast(bf16[32,32,128]{2,1,0:T(8,128)(2,1)S(1)} %all-to-all-done.3), dimensions={0,1,3} | broadcast | bytes 2359296 | tf_op jit(solution)/shard_map/mul | solution.py:124
  117.6 29.1 %scatter_custom_fusion.3 = f32[2048,128]{1,0:T(8,128)S(1)} fusion(s32[4096]{0:T(1024)} %bitcast.287, f32[4096,128]{1,0:T(8,128)} %bitcast.243, f32[4096]{0:T(1024)S(1)} %mul.81, f32[]{:T(128)} %constant.6.clone.1), kind=kCustom, calls=%fused_computation.41 | custom fusion | flops 1048576 | bytes 3162624 | tf_op jit(solution)/shard_map/scatter-add | solution.py:128
  146.8 4.1 %collective-permute-start.4 = (bf16[1,512,128]{2,1,0:T(8,128)(2,1)S(1)}, bf16[1,512,128]{2,1,0:T(8,128)(2,1)S(1)}, u32[]{:S(2)}, u32[]{:S(2)}) collective-permute-start(bf16[1,512,128]{2,1,0:T(8,128)(2,1)S(1)} %get-tuple-element.64), channel_id=1, source_target_pairs={{0,1},{1,2},{2,3},{3,4},{4,5},{5,6},{6,7},{7,8},{8,9},{9,10},{10,1... | collective-permute-start | bytes 393224 | tf_op jit(solution)/shard_map/ppermute | solution.py:12
  150.9 1.9 %collective-permute-start.5 = (bf16[1,512,128]{2,1,0:T(8,128)(2,1)S(1)}, bf16[1,512,128]{2,1,0:T(8,128)(2,1)S(1)}, u32[]{:S(2)}, u32[]{:S(2)}) collective-permute-start(bf16[1,512,128]{2,1,0:T(8,128)(2,1)S(1)} %get-tuple-element.63), channel_id=1, source_target_pairs={{1,0},{2,1},{3,2},{4,3},{5,4},{6,5},{7,6},{8,7},{9,8},{10,9},{11,1... | collective-permute-start | bytes 393224 | tf_op jit(solution)/shard_map/ppermute | solution.py:15
  152.9 6.1 %collective-permute-done.5 = bf16[1,512,128]{2,1,0:T(8,128)(2,1)S(1)} collective-permute-done((bf16[1,512,128]{2,1,0:T(8,128)(2,1)S(1)}, bf16[1,512,128]{2,1,0:T(8,128)(2,1)S(1)}, u32[]{:S(2)}, u32[]{:S(2)}) %collective-permute-start.5) | collective-permute-done | bytes 131104 | tf_op jit(solution)/shard_map/ppermute | solution.py:15
  159.6 0.5 fusion.37
  163.9 1.9 %collective-permute-start.6 = (bf16[1,512,128]{2,1,0:T(8,128)(2,1)S(1)}, bf16[1,512,128]{2,1,0:T(8,128)(2,1)S(1)}, u32[]{:S(2)}, u32[]{:S(2)}) collective-permute-start(bf16[1,512,128]{2,1,0:T(8,128)(2,1)S(1)} %get-tuple-element.53), channel_id=1, source_target_pairs={{0,1},{1,2},{2,3},{3,4},{4,5},{5,6},{6,7},{7,8},{8,9},{9,10},{10,1... | collective-permute-start | bytes 393224 | tf_op jit(solution)/shard_map/ppermute | solution.py:12
  165.9 2.4 %collective-permute-start.7 = (bf16[1,512,128]{2,1,0:T(8,128)(2,1)S(1)}, bf16[1,512,128]{2,1,0:T(8,128)(2,1)S(1)}, u32[]{:S(2)}, u32[]{:S(2)}) collective-permute-start(bf16[1,512,128]{2,1,0:T(8,128)(2,1)S(1)} %get-tuple-element.52), channel_id=1, source_target_pairs={{1,0},{2,1},{3,2},{4,3},{5,4},{6,5},{7,6},{8,7},{9,8},{10,9},{11,1... | collective-permute-start | bytes 393224 | tf_op jit(solution)/shard_map/ppermute | solution.py:15
  168.3 5.6 %collective-permute-done.7 = bf16[1,512,128]{2,1,0:T(8,128)(2,1)S(1)} collective-permute-done((bf16[1,512,128]{2,1,0:T(8,128)(2,1)S(1)}, bf16[1,512,128]{2,1,0:T(8,128)(2,1)S(1)}, u32[]{:S(2)}, u32[]{:S(2)}) %collective-permute-start.7) | collective-permute-done | bytes 131104 | tf_op jit(solution)/shard_map/ppermute | solution.py:15
  174.6 0.5 fusion.33
  178.0 0.9 copy-done.3
  179.1 1.1 multiply_add_fusion
  (123 shorter events, 18.8 us)
Async XLA Ops:
  0.0 93.6 %copy-start = (f32[616,616]{1,0:T(8,128)S(1)}, f32[616,616]{1,0:T(8,128)}, u32[]{:S(2)}) copy-start(f32[616,616]{1,0:T(8,128)} %param.31) | copy-start | bytes 4553476
  0.0 7.1 %copy-start.11 = (s32[512,1]{0,1:T(1,128)S(1)}, s32[512,1]{0,1:T(1,128)}, u32[]{:S(2)}) copy-start(s32[512,1]{0,1:T(1,128)} %param.22) | copy-start | bytes 6148
  0.0 8.7 %copy-start.12 = (s32[512,4]{0,1:T(4,128)S(1)}, s32[512,4]{0,1:T(4,128)}, u32[]{:S(2)}) copy-start(s32[512,4]{0,1:T(4,128)} %param.23) | copy-start | bytes 24580
  1.4 16.5 %copy-start.13 = (f32[512,4]{0,1:T(4,128)S(1)}, f32[512,4]{0,1:T(4,128)}, u32[]{:S(2)}) copy-start(f32[512,4]{0,1:T(4,128)} %param.24) | copy-start | bytes 24580
  1.5 32.3 %collective-permute-start = (bf16[1,512,128]{2,1,0:T(8,128)(2,1)S(1)}, bf16[1,512,128]{2,1,0:T(8,128)(2,1)S(1)}, u32[]{:S(2)}, u32[]{:S(2)}) collective-permute-start(bf16[1,512,128]{2,1,0:T(8,128)(2,1)S(1)} %get-tuple-element.86), channel_id=1, source_target_pairs={{0,1},{1,2},{2,3},{3,4},{4,5},{5,6},{6,7},{7,8},{8,9},{9,10},{10,1... | collective-permute-start | bytes 393224 | tf_op jit(solution)/shard_map/ppermute | solution.py:12
  5.2 28.6 %collective-permute-start.1 = (bf16[1,512,128]{2,1,0:T(8,128)(2,1)S(1)}, bf16[1,512,128]{2,1,0:T(8,128)(2,1)S(1)}, u32[]{:S(2)}, u32[]{:S(2)}) collective-permute-start(bf16[1,512,128]{2,1,0:T(8,128)(2,1)S(1)} %get-tuple-element.85), channel_id=1, source_target_pairs={{1,0},{2,1},{3,2},{4,3},{5,4},{6,5},{7,6},{8,7},{9,8},{10,9},{11,1... | collective-permute-start | bytes 393224 | tf_op jit(solution)/shard_map/ppermute | solution.py:15
  11.7 10.0 %all-to-all-start = ((s32[32,1,128]{2,1,0:T(1,128)}), s32[32,1,128]{2,1,0:T(1,128)S(1)}, u32[]{:S(2)}, u32[]{:S(2)}) async-start(s32[32,1,128]{2,1,0:T(1,128)} %reshape.297), calls=%async_computation | async-start | bytes 32768 | tf_op jit(solution)/shard_map/all_to_all | solution.py:93
  21.7 9.7 %all-to-all-start.1 = ((f32[32,1,128]{2,1,0:T(1,128)}), f32[32,1,128]{2,1,0:T(1,128)S(1)}, u32[]{:S(2)}, u32[]{:S(2)}) async-start(f32[32,1,128]{2,1,0:T(1,128)} %reshape.299), calls=%async_computation.1 | async-start | bytes 32768 | tf_op jit(solution)/shard_map/all_to_all | solution.py:98
  29.4 4.8 %copy-start.10 = (s32[4096,1]{0,1:T(1,128)}, s32[4096,1]{0,1:T(1,128)S(1)}, u32[]{:S(2)}) copy-start(s32[4096,1]{0,1:T(1,128)S(1)} %compare_select_fusion) | copy-start | bytes 49156
  34.3 1.6 copy-start.6
  38.2 0.7 copy-start.14
  39.0 6.7 %collective-permute-start.2 = (bf16[1,512,128]{2,1,0:T(8,128)(2,1)S(1)}, bf16[1,512,128]{2,1,0:T(8,128)(2,1)S(1)}, u32[]{:S(2)}, u32[]{:S(2)}) collective-permute-start(bf16[1,512,128]{2,1,0:T(8,128)(2,1)S(1)} %get-tuple-element.75), channel_id=1, source_target_pairs={{0,1},{1,2},{2,3},{3,4},{4,5},{5,6},{6,7},{7,8},{8,9},{9,10},{10,1... | collective-permute-start | bytes 393224 | tf_op jit(solution)/shard_map/ppermute | solution.py:12
  43.6 8.1 %collective-permute-start.3 = (bf16[1,512,128]{2,1,0:T(8,128)(2,1)S(1)}, bf16[1,512,128]{2,1,0:T(8,128)(2,1)S(1)}, u32[]{:S(2)}, u32[]{:S(2)}) collective-permute-start(bf16[1,512,128]{2,1,0:T(8,128)(2,1)S(1)} %get-tuple-element.74), channel_id=1, source_target_pairs={{1,0},{2,1},{3,2},{4,3},{5,4},{6,5},{7,6},{8,7},{9,8},{10,9},{11,1... | collective-permute-start | bytes 393224 | tf_op jit(solution)/shard_map/ppermute | solution.py:15
  52.3 1.0 copy-start.5
  55.6 1.2 copy-start.2
  72.0 16.6 %copy-start.17 = (f32[1024]{0:T(1024)S(1)}, f32[1024]{0:T(1024)}, u32[]{:S(2)}) copy-start(f32[1024]{0:T(1024)} %param.28) | copy-start | bytes 12292
  76.1 15.0 %copy-start.18 = (f32[616]{0:T(1024)S(1)}, f32[616]{0:T(1024)}, u32[]{:S(2)}) copy-start(f32[616]{0:T(1024)} %param.30) | copy-start | bytes 7396
  76.1 11.2 %all-to-all-start.2 = ((bf16[32,32,128]{2,1,0:T(8,128)(2,1)}), bf16[32,32,128]{2,1,0:T(8,128)(2,1)S(1)}, u32[]{:S(2)}, u32[]{:S(2)}) async-start(bf16[32,32,128]{2,1,0:T(8,128)(2,1)} %fusion.1), calls=%async_computation.2 | async-start | bytes 524288 | tf_op jit(solution)/shard_map/all_to_all | solution.py:102
  90.1 1.0 copy-start.19
  100.0 8.9 %copy-start.7 = (bf16[3,3,128,128]{3,2,1,0:T(8,128)(2,1)S(1)}, bf16[3,3,128,128]{3,2,1,0:T(8,128)(2,1)}, u32[]{:S(2)}) copy-start(bf16[3,3,128,128]{3,2,1,0:T(8,128)(2,1)} %param.19) | copy-start | bytes 884740
  100.0 8.9 %copy-start.4 = (f32[32,32,4]{2,1,0:T(8,128)S(1)}, f32[32,32,4]{2,1,0:T(8,128)}, u32[]{:S(2)}) copy-start(f32[32,32,4]{2,1,0:T(8,128)} %copy.26) | copy-start | bytes 49156
  102.6 13.2 %all-to-all-start.3 = ((bf16[32,32,128]{2,1,0:T(8,128)(2,1)}), bf16[32,32,128]{2,1,0:T(8,128)(2,1)S(1)}, u32[]{:S(2)}, u32[]{:S(2)}) async-start(bf16[32,32,128]{2,1,0:T(8,128)(2,1)} %bitcast.49), calls=%async_computation.3 | async-start | bytes 524288 | tf_op jit(solution)/shard_map/all_to_all | solution.py:117
  146.8 6.1 %collective-permute-start.4 = (bf16[1,512,128]{2,1,0:T(8,128)(2,1)S(1)}, bf16[1,512,128]{2,1,0:T(8,128)(2,1)S(1)}, u32[]{:S(2)}, u32[]{:S(2)}) collective-permute-start(bf16[1,512,128]{2,1,0:T(8,128)(2,1)S(1)} %get-tuple-element.64), channel_id=1, source_target_pairs={{0,1},{1,2},{2,3},{3,4},{4,5},{5,6},{6,7},{7,8},{8,9},{9,10},{10,1... | collective-permute-start | bytes 393224 | tf_op jit(solution)/shard_map/ppermute | solution.py:12
  150.9 8.1 %collective-permute-start.5 = (bf16[1,512,128]{2,1,0:T(8,128)(2,1)S(1)}, bf16[1,512,128]{2,1,0:T(8,128)(2,1)S(1)}, u32[]{:S(2)}, u32[]{:S(2)}) collective-permute-start(bf16[1,512,128]{2,1,0:T(8,128)(2,1)S(1)} %get-tuple-element.63), channel_id=1, source_target_pairs={{1,0},{2,1},{3,2},{4,3},{5,4},{6,5},{7,6},{8,7},{9,8},{10,9},{11,1... | collective-permute-start | bytes 393224 | tf_op jit(solution)/shard_map/ppermute | solution.py:15
  159.6 1.0 copy-start.8
  163.0 0.7 copy-start.15
  163.9 4.4 %collective-permute-start.6 = (bf16[1,512,128]{2,1,0:T(8,128)(2,1)S(1)}, bf16[1,512,128]{2,1,0:T(8,128)(2,1)S(1)}, u32[]{:S(2)}, u32[]{:S(2)}) collective-permute-start(bf16[1,512,128]{2,1,0:T(8,128)(2,1)S(1)} %get-tuple-element.53), channel_id=1, source_target_pairs={{0,1},{1,2},{2,3},{3,4},{4,5},{5,6},{6,7},{7,8},{8,9},{9,10},{10,1... | collective-permute-start | bytes 393224 | tf_op jit(solution)/shard_map/ppermute | solution.py:12
  165.9 8.1 %collective-permute-start.7 = (bf16[1,512,128]{2,1,0:T(8,128)(2,1)S(1)}, bf16[1,512,128]{2,1,0:T(8,128)(2,1)S(1)}, u32[]{:S(2)}, u32[]{:S(2)}) collective-permute-start(bf16[1,512,128]{2,1,0:T(8,128)(2,1)S(1)} %get-tuple-element.52), channel_id=1, source_target_pairs={{1,0},{2,1},{3,2},{4,3},{5,4},{6,5},{7,6},{8,7},{9,8},{10,9},{11,1... | collective-permute-start | bytes 393224 | tf_op jit(solution)/shard_map/ppermute | solution.py:15
  177.6 1.2 copy-start.3
  177.6 1.5 copy-start.9
  177.6 1.5 copy-start.16
  177.9 2.3 %copy-start.1 = (f32[616,616]{1,0:T(8,128)S(1)}, f32[616,616]{1,0:T(8,128)}, u32[]{:S(2)}) copy-start(f32[616,616]{1,0:T(8,128)} %param.31) | copy-start | bytes 4553476
where the time goes:
time: 181 us; the launch traced here: 180 us
  other arithmetic  45.2 us (25%)
  starting transfers between devices  43.9 us (24%)
  local copies, waits for them, and re-layouts  35 us (19%)
  waiting for transfers between devices  34 us (19%)
  matrix products  20.7 us (11%)
    scatter-add x1, other arithmetic, per_device(): obs_grad = jnp.zeros((tile_rows * tile_cols, channels), jnp.float32).at[r...  29.1 us
    ppermute x4, waiting for transfers between devices, padded_2(): lax.ppermute(lax.slice_in_dim(block, 0, width, axis=dim), axis, backward)  17.7 us
    gather x1, local copies, waits for them, and re-layouts, per_device(): observed_flat[requested.reshape(-1)]  15 us
    ppermute x4, starting transfers between devices, padded_2(): lax.ppermute(lax.slice_in_dim(block, block.shape[dim] - width, None, axis...  14.3 us
    dot_general x36, matrix products, conv_rows(): jnp.dot(shifted.reshape(-1, channels), kernel[row_off, col_off], preferre...  10.4 us
    ppermute x4, starting transfers between devices, padded_2(): lax.ppermute(lax.slice_in_dim(block, 0, width, axis=dim), axis, backward)  8.35 us
    all_to_all x1, waiting for transfers between devices, per_device(): lax.all_to_all(blended, 'dev', split_axis=0, concat_axis=0, tiled=True)  6.91 us
    unnamed x46, local copies, waits for them, and re-layouts  6.65 us
  transfers between devices with their start and end apart: 12, of which 7 were waited for; matrix products, arithmetic and copies ran while one was open for 7% of the time, Pallas kernels for 0%

commit v1 on v0

v1 whole, which is shorter than its diff:
```python
import functools

import jax
import jax.numpy as jnp
from jax import lax
from jax.experimental import pallas as pl
from jax.experimental.pallas import tpu as pltpu
from jax.sharding import PartitionSpec as P

F32 = jnp.float32
BF16 = jnp.bfloat16
MESH = pl.DeviceIdType.MESH
LANES = 128


def dot(a, b):
    return jnp.dot(a, b, preferred_element_type=F32)


def dot_nt(a, b):
    return lax.dot_general(a, b, (((1,), (1,)), ((), ())), preferred_element_type=F32)


def kernel(
    n,
    table_ref,
    live_ref,
    back_precision_ref,
    bias_first_ref,
    bias_in_ref,
    bias_out_ref,
    state_hbm,
    background_hbm,
    conv_first_hbm,
    conv_second_hbm,
    observations_hbm,
    layer_in_hbm,
    layer_out_hbm,
    precision_hbm,
    out_ref,
    state_ref,
    background_ref,
    conv_first_ref,
    conv_second_ref,
    adj_first_ref,
    adj_second_ref,
    observations_ref,
    layer_in_ref,
    layer_out_ref,
    precision_ref,
    field_ref,
    halo_ref,
    taps_ref,
    hidden_ref,
    hidden_taps_ref,
    observed_t_ref,
    place_ref,
    place_t_ref,
    share_t_ref,
    grad_ref,
    req_src,
    req_dst,
    ret_src,
    ret_dst,
    out_src,
    out_dst,
    load_sem,
    halo_send,
    halo_recv,
    req_send,
    req_recv,
    ret_send,
    ret_recv,
    out_send,
    out_recv,
):
    me = lax.axis_index("dev")
    rows, cols, ch = state_ref.shape
    slots = place_t_ref.shape[0]
    listed = place_t_ref.shape[1]
    cap = slots // n
    per = LANES // cap
    groups = slots // LANES
    up = lax.rem(me + n - 1, n)
    down = lax.rem(me + 1, n)

    loads = [
        pltpu.make_async_copy(src, dst, load_sem.at[i])
        for i, (src, dst) in enumerate(
            (
                (state_hbm, state_ref),
                (conv_first_hbm, conv_first_ref),
                (conv_second_hbm, conv_second_ref),
                (layer_in_hbm, layer_in_ref),
                (layer_out_hbm, layer_out_ref),
                (observations_hbm, observations_ref),
                (precision_hbm, precision_ref),
                (background_hbm, background_ref),
            )
        )
    ]
    for load in loads:
        load.start()

    barrier = pltpu.get_barrier_semaphore()

    def greet(k, carry):
        pl.semaphore_signal(
            barrier, inc=1, device_id=(lax.rem(me + k, n),), device_id_type=MESH
        )
        return carry

    lax.fori_loop(1, n, greet, 0)

    def exchange(src, dst, send, recv):
        def start(k, carry):
            target = lax.rem(me + k, n)
            pltpu.make_async_remote_copy(
                src_ref=src.at[target],
                dst_ref=dst.at[me],
                send_sem=send.at[k],
                recv_sem=recv.at[k],
                device_id=(target,),
                device_id_type=MESH,
            ).start()
            return carry

        lax.fori_loop(1, n, start, 0)

    def settle(src, dst, send, recv):
        def wait(k, carry):
            copy = pltpu.make_async_remote_copy(
                src_ref=src.at[lax.rem(me + k, n)],
                dst_ref=dst.at[lax.rem(me + n - k, n)],
                send_sem=send.at[k],
                recv_sem=recv.at[k],
                device_id=(lax.rem(me + k, n),),
                device_id_type=MESH,
            )
            copy.wait_recv()
            copy.wait_send()
            return carry

        lax.fori_loop(1, n, wait, 0)

    def rim(phase):
        return [
            pltpu.make_async_remote_copy(
                src_ref=field_ref.at[phase, pl.ds(rows - 2 if side == 0 else 0, 2)],
                dst_ref=halo_ref.at[phase, side],
                send_sem=halo_send.at[phase, side],
                recv_sem=halo_recv.at[phase, side],
                device_id=(down if side == 0 else up,),
                device_id_type=MESH,
            )
            for side in range(2)
        ]

    def put_taps(taps, row, value):
        taps[row, :, pl.ds(0, ch)] = pltpu.roll(value, 1, 0).astype(BF16)
        taps[row, :, pl.ds(ch, ch)] = value.astype(BF16)
        taps[row, :, pl.ds(2 * ch, ch)] = pltpu.roll(value, cols - 1, 0).astype(BF16)

    def conv_row(taps, row, weights):
        return (
            dot(taps[row], weights[0])
            + dot(taps[row + 1], weights[1])
            + dot(taps[row + 2], weights[2])
        )

    def put_halo(phase):
        for side in range(2):
            inside = (me > 0) if side == 0 else (me < n - 1)
            for i in range(2):
                value = halo_ref[phase, side, i].astype(F32) * inside.astype(F32)
                put_taps(taps_ref, i if side == 0 else rows + 2 + i, value)

    def within(row):
        first, last = me == 0, me == n - 1
        return 1.0 - jnp.where(
            (first & (row == 0)) | (last & (row == rows + 1)), 1.0, 0.0
        ).astype(F32)

    loads[0].wait()

    def take_state(r, carry):
        field_ref[0, r] = state_ref[r].astype(BF16)
        return carry

    lax.fori_loop(0, rows, take_state, 0)

    table = table_ref[...]
    tile_row = table[8:9]
    tile_col = jnp.broadcast_to(tile_row, (LANES, listed)).T[:, 0:1]
    same = tile_col == tile_row
    from_col = lax.broadcasted_iota(jnp.int32, (listed, listed), 0)
    from_row = lax.broadcasted_iota(jnp.int32, (listed, listed), 1)
    rank_row = jnp.sum(jnp.where(same & (from_col < from_row), 1.0, 0.0), axis=0, keepdims=True)
    rank_col = jnp.sum(jnp.where(same & (from_row < from_col), 1.0, 0.0), axis=1, keepdims=True)
    slot_row = (tile_row * cap + rank_row).astype(jnp.int32)
    slot_col = (tile_col * cap + rank_col).astype(jnp.int32)
    for g in range(groups):
        rowid = lax.broadcasted_iota(jnp.int32, (LANES, listed), 0) + g * LANES
        place_t_ref[pl.ds(g * LANES, LANES)] = jnp.where(rowid == slot_row, 1.0, 0.0).astype(BF16)
        colid = lax.broadcasted_iota(jnp.int32, (listed, LANES), 1) + g * LANES
        place_ref[:, pl.ds(g * LANES, LANES)] = jnp.where(colid == slot_col, 1.0, 0.0).astype(BF16)

    values = table[0:8]
    part_1 = values.astype(BF16).astype(F32)
    part_2 = (values - part_1).astype(BF16).astype(F32)
    part_3 = values - part_1 - part_2
    parts = jnp.concatenate([part_1, part_2, part_3, jnp.zeros_like(values)], axis=0).astype(BF16)
    own_lanes = lax.broadcasted_iota(jnp.int32, (8, LANES), 1) // cap == lax.rem(me, per)
    for g in range(groups):
        spread = dot_nt(parts, place_t_ref[pl.ds(g * LANES, LANES)])
        spread = spread[0:8] + spread[8:16] + spread[16:24]
        for i in range(per):
            turned = pltpu.roll(spread, lax.rem(lax.rem(me, per) + per - i, per) * cap, 1)
            req_src[g * per + i] = jnp.where(own_lanes, turned, 0.0)
    req_dst[me] = req_src[me]

    pl.semaphore_wait(barrier, n - 1)
    forward_rim = rim(0)
    for copy in forward_rim:
        copy.start()
    exchange(req_src, req_dst, req_send, req_recv)

    def take_taps(r, carry):
        put_taps(taps_ref, r + 2, state_ref[r].astype(BF16).astype(F32))
        return carry

    lax.fori_loop(0, rows, take_taps, 0)
    loads[1].wait()
    loads[2].wait()
    for kernel_ref, adj_ref in ((conv_first_ref, adj_first_ref), (conv_second_ref, adj_second_ref)):
        for a in range(3):
            for b in range(3):
                tap = kernel_ref[2 - a, pl.ds((2 - b) * ch, ch)].astype(F32)
                adj_ref[a, pl.ds(b * ch, ch)] = tap.T.astype(BF16)

    def forward_row(row, carry):
        value = jnp.tanh(conv_row(taps_ref, row, conv_first_ref) + bias_first_ref[...])
        value = value.astype(BF16).astype(F32) * within(row)
        hidden_ref[row] = value
        put_taps(hidden_taps_ref, row, value)
        return carry

    lax.fori_loop(2, rows, forward_row, 0)
    for copy in forward_rim:
        copy.wait_recv()
    put_halo(0)
    lax.fori_loop(0, 2, forward_row, 0)
    lax.fori_loop(rows, rows + 2, forward_row, 0)

    def observed_row(r, carry):
        value = state_ref[r] + conv_row(hidden_taps_ref, r, conv_second_ref)
        observed_t_ref[:, pl.ds(pl.multiple_of(r * cols, LANES), cols)] = value.T.astype(BF16)
        return carry

    lax.fori_loop(0, rows, observed_row, 0)

    settle(req_src, req_dst, req_send, req_recv)
    wanted = []
    for g in range(groups):
        total = req_dst[g * per]
        for i in range(1, per):
            total = total + req_dst[g * per + i]
        wanted.append(total)
    margin = 4

    def build_shares(c, carry):
        base = pl.multiple_of(c * LANES, LANES)
        cell = (lax.broadcasted_iota(jnp.int32, (LANES, LANES), 0) + base).astype(F32)
        for g in range(groups):
            total = jnp.zeros((LANES, LANES), F32)
            for k in range(margin):
                total = total + jnp.where(
                    cell == wanted[g][k : k + 1], wanted[g][margin + k : margin + k + 1], 0.0
                )
            share_t_ref[pl.ds(base, LANES), pl.ds(g * LANES, LANES)] = total.astype(BF16)
        return carry

    lax.fori_loop(0, rows * cols // LANES, build_shares, 0)

    def blend(g, carry):
        width = 2 * LANES
        base = pl.multiple_of(g * width, width)
        blended = dot(observed_t_ref[...], share_t_ref[:, pl.ds(base, width)]).T
        ret_src[pl.ds(g * (width // cap), width // cap)] = blended.reshape(
            width // cap, cap, ch
        ).astype(BF16)
        return carry

    lax.fori_loop(0, groups // 2, blend, 0)
    ret_dst[me] = ret_src[me]
    exchange(ret_src, ret_dst, ret_send, ret_recv)
    for load in loads[3:7]:
        load.wait()
    precision = precision_ref[...].astype(BF16)
    settle(ret_src, ret_dst, ret_send, ret_recv)
    returned = ret_dst[...].astype(F32).reshape(slots, ch).astype(BF16)
    live = live_ref[0]
    block = listed // 4
    for s in range(0, listed, block):
        span = pl.ds(s, block)
        interpolated = dot(place_ref[span], returned).astype(BF16)
        activated = jnp.tanh(dot(interpolated, layer_in_ref[...]) + bias_in_ref[...]).astype(BF16)
        radiance = dot(activated, layer_out_ref[...]) + bias_out_ref[...]
        alive = lax.broadcasted_iota(jnp.int32, (block, 1), 0) + s < live
        innovation = jnp.where(alive, radiance - observations_ref[span], 0.0)
        weighted = dot(innovation.astype(BF16), precision)
        back_act = dot_nt(weighted.astype(BF16), layer_out_ref[...])
        act_wide = activated.astype(F32)
        pre_grad = (back_act * (1.0 - act_wide * act_wide)).astype(BF16)
        grad_ref[span] = dot_nt(pre_grad, layer_in_ref[...]).astype(BF16)

    def dispatch(g, carry):
        width = 2 * LANES
        base = pl.multiple_of(g * width, width)
        outgoing = dot(place_t_ref[pl.ds(base, width)], grad_ref[...])
        out_src[pl.ds(g * (width // cap), width // cap)] = outgoing.reshape(
            width // cap, cap, ch
        ).astype(BF16)
        return carry

    lax.fori_loop(0, groups // 2, dispatch, 0)
    out_dst[me] = out_src[me]
    exchange(out_src, out_dst, out_send, out_recv)
    settle(out_src, out_dst, out_send, out_recv)
    arrived = out_dst[...].astype(F32).reshape(slots, ch).astype(BF16)

    def gather_grad(r, carry):
        value = dot(share_t_ref[pl.ds(pl.multiple_of(r * cols, LANES), cols)], arrived)
        out_ref[r] = value
        field_ref[1, r] = value.astype(BF16)
        return carry

    lax.fori_loop(0, rows, gather_grad, 0)
    for copy in forward_rim:
        copy.wait_send()
    backward_rim = rim(1)
    for copy in backward_rim:
        copy.start()

    def take_grad(r, carry):
        put_taps(taps_ref, r + 2, out_ref[r].astype(BF16).astype(F32))
        return carry

    lax.fori_loop(0, rows, take_grad, 0)

    def backward_row(row, carry):
        value = conv_row(taps_ref, row, adj_second_ref)
        hidden = hidden_ref[row]
        value = value * (1.0 - hidden * hidden) * within(row)
        put_taps(hidden_taps_ref, row, value.astype(BF16).astype(F32))
        return carry

    lax.fori_loop(2, rows, backward_row, 0)
    for copy in backward_rim:
        copy.wait_recv()
    put_halo(1)
    lax.fori_loop(0, 2, backward_row, 0)
    lax.fori_loop(rows, rows + 2, backward_row, 0)
    loads[7].wait()

    def last_row(r, carry):
        out_ref[r] = (
            out_ref[r]
            + conv_row(hidden_taps_ref, r, adj_first_ref)
            + back_precision_ref[...] * (state_ref[r] - background_ref[r])
        )
        return carry

    lax.fori_loop(0, rows, last_row, 0)
    for copy in backward_rim:
        copy.wait_send()


def per_device(
    state,
    background,
    back_precision,
    conv_first,
    bias_first,
    conv_second,
    sounding_tile,
    sounding_cells,
    cell_weights,
    observations,
    live_counts,
    layer_in,
    bias_in,
    layer_out,
    bias_out,
    error_precision,
):
    rows, cols, ch = state.shape
    n = lax.axis_size("dev")
    listed = sounding_tile.shape[0]
    slots = 2 * listed
    cap = slots // n
    hid, chan = layer_out.shape
    table = jnp.concatenate(
        [
            sounding_cells.T.astype(F32),
            cell_weights.T,
            jnp.broadcast_to(sounding_tile.reshape(1, listed).astype(F32), (8, listed)),
        ],
        axis=0,
    )
    vmem = pl.BlockSpec(memory_space=pltpu.VMEM)
    hbm = pl.BlockSpec(memory_space=pl.ANY)
    dma = pltpu.SemaphoreType.DMA
    return pl.pallas_call(
        functools.partial(kernel, n),
        out_shape=jax.ShapeDtypeStruct(state.shape, F32),
        in_specs=[vmem, pl.BlockSpec(memory_space=pltpu.SMEM)] + [vmem] * 4 + [hbm] * 8,
        out_specs=vmem,
        scratch_shapes=[
            pltpu.VMEM(state.shape, F32),
            pltpu.VMEM(state.shape, F32),
            pltpu.VMEM((3, 3 * ch, ch), BF16),
            pltpu.VMEM((3, 3 * ch, ch), BF16),
            pltpu.VMEM((3, 3 * ch, ch), BF16),
            pltpu.VMEM((3, 3 * ch, ch), BF16),
            pltpu.VMEM((listed, chan), F32),
            pltpu.VMEM((ch, hid), BF16),
            pltpu.VMEM((hid, chan), BF16),
            pltpu.VMEM((chan, chan), F32),
            pltpu.VMEM((2, rows, cols, ch), BF16),
            pltpu.VMEM((2, 2, 2, cols, ch), BF16),
            pltpu.VMEM((rows + 4, cols, 3 * ch), BF16),
            pltpu.VMEM((rows + 2, cols, ch), F32),
            pltpu.VMEM((rows + 2, cols, 3 * ch), BF16),
            pltpu.VMEM((ch, rows * cols), BF16),
            pltpu.VMEM((listed, slots), BF16),
            pltpu.VMEM((slots, listed), BF16),
            pltpu.VMEM((rows * cols, slots), BF16),
            pltpu.VMEM((listed, ch), BF16),
            pltpu.VMEM((n, 8, LANES), F32),
            pltpu.VMEM((n, 8, LANES), F32),
            pltpu.VMEM((n, cap, ch), BF16),
            pltpu.VMEM((n, cap, ch), BF16),
            pltpu.VMEM((n, cap, ch), BF16),
            pltpu.VMEM((n, cap, ch), BF16),
            dma((8,)),
            dma((2, 2)),
            dma((2, 2)),
            dma((n,)),
            dma((n,)),
            dma((n,)),
            dma((n,)),
            dma((n,)),
            dma((n,)),
        ],
        compiler_params=pltpu.CompilerParams(
            collective_id=0, has_side_effects=True, vmem_limit_bytes=60 * 1024 * 1024
        ),
        name="step",
    )(
        table,
        live_counts,
        back_precision.reshape(1, -1),
        bias_first.reshape(1, -1),
        bias_in.reshape(1, -1),
        bias_out.reshape(1, -1),
        state,
        background,
        conv_first.reshape(3, 3 * ch, ch),
        conv_second.reshape(3, 3 * ch, ch),
        observations,
        layer_in,
        layer_out,
        error_precision,
    )


def solution(mesh):
    return jax.shard_map(
        per_device,
        mesh=mesh,
        in_specs=(
            P("dev", None, None),
            P("dev", None, None),
            P(),
            P(),
            P(),
            P(),
            P("dev", None),
            P("dev", None),
            P("dev", None),
            P("dev", None),
            P("dev"),
            P(),
            P(),
            P(),
            P(),
            P(),
        ),
        out_specs=P("dev", None, None),
        check_vma=False,
    )
```

time: 181 us -> 75.5 us (0.42)
  the two profiles are of different devices: /device:TPU:15 before, /device:TPU:0 now
where the time goes in v1:
time: 75.5 us; the launch traced here: 75.1 us
  Pallas kernels  63.9 us (85%)
  local copies, waits for them, and re-layouts  7.76 us (10%)
  other arithmetic  2.8 us (4%)
    pallas_call x1, Pallas kernels, per_device(): pl.pallas_call(functools.partial(kernel, n), out_shape=jax.ShapeDtypeStru...  63.9 us
    unnamed x5, local copies, waits for them, and re-layouts  6.48 us

profile of v1, /device:TPU:0, one launch (start us, length us, event | category | flops | bytes accessed | tf_op | source)
XLA Modules:
  0.0 75.1 jit_solution(9716629148661953551)
XLA Ops:
  0.7 0.7 convert_element_type.19
  1.3 1.3 %reshape.30.bias_out_ref = f32[1,616]{1,0:T(1,128)} reshape(f32[616]{0:T(1024)} %param.30) | data formatting | bytes 4928 | tf_op jit(solution)/shard_map/reshape | solution.py:466
  2.6 0.7 convert_bitcast_fusion
  3.3 0.0 copy-start
  3.3 1.4 %pad_maximum_fusion.table_ref = f32[16,512]{1,0:T(8,128)} fusion(f32[8,512]{1,0:T(8,128)S(1)} %broadcast_in_dim.2, f32[4,512]{1,0:T(4,128)} %bitcast.12, f32[4,512]{1,0:T(4,128)S(1)} %convert_bitcast_fusion), kind=kLoop, calls=%fused_computation | loop fusion | flops 16384 | bytes 65536 | tf_op jit(solution)/shard_map/concatenate | solution.py:403
  4.7 2.8 %copy.17.observations_hbm = f32[512,616]{1,0:T(8,128)} copy(f32[512,616]{0,1:T(8,128)} %param.25) | data formatting | bytes 2523136 | tf_op args[9]
  7.5 0.0 copy-done
  7.5 1.4 %copy.18.layer_out_hbm = bf16[1024,616]{1,0:T(8,128)(2,1)} copy(bf16[1024,616]{0,1:T(8,128)(2,1)S(1)} %copy-done) | data formatting | bytes 2523136 | tf_op args[13]
  9.0 63.9 %step.1 = f32[4,512,128]{2,1,0:T(8,128)} custom-call(f32[16,512]{1,0:T(8,128)} %pad_maximum_fusion.table_ref, s32[1]{0:T(128)S(6)} %copy.20.live_ref, f32[1,128]{1,0:T(1,128)} %bitcast.14, f32[1,128]{1,0:T(1,128)} %bitcast.15, f32[1,1024]{1,0:T(1,128)} %bitcast.13, f32[1,616]{1,0:T(1,128)} %reshape.30.bias_out_ref, f32[4,512,128]{2,1,0:T(8,128)} %state_hbm.1, ...), custom_call_target="tpu_custom_call" | custom-call | tf_op jit(solution)/shard_map/step/pallas_call | solution.py:414
  72.8 2.3 %copy.21 = f32[4,512,128]{2,1,0:T(8,128)} copy(f32[4,512,128]{2,1,0:T(8,128)} %step.1) | data formatting | bytes 2097152
  (1 shorter events, 0.0 us)
Async XLA Ops:
  3.3 4.2 %copy-start = (bf16[1024,616]{0,1:T(8,128)(2,1)S(1)}, bf16[1024,616]{0,1:T(8,128)(2,1)}, u32[]{:S(2)}) copy-start(bf16[1024,616]{0,1:T(8,128)(2,1)} %param.29) | copy-start | bytes 3784708
